TPU v7x, 32 devices: a whole 2x2x4 slice. The times are simulated.
32 devices in a mesh: rp: 2 (over x), pb: 16 (over z, y, core).
Axes of the slice: x: 2, y: 2, z: 4, core: 2. Of those that a mesh axis runs over, the one named last changes fastest.
Arguments:
- wannier_g: bfloat16 [2, 1024, 32, 1152], P(None, 'rp', 'pb'), may hold values from -0.19921875 to 0.19921875
- rp_coords: int32 [3, 1024], replicated, may hold values from -8 to 8
- q_coords: int32 [3, 64], P(None, ('rp', 'pb')), may hold values from 0 to 15
- k_index: int32 [1], replicated, may hold values from 0 to 7
- k_vectors: bfloat16 [8, 2, 32, 32], replicated, may hold values from -0.75 to 0.75
- kq_vectors: bfloat16 [64, 2, 32, 32], P(('rp', 'pb')), may hold values from -0.75 to 0.75
- modes: bfloat16 [64, 2, 36, 36], P(('rp', 'pb')), may hold values from -0.75 to 0.75
Outputs:
- rotated: float32 [64, 2, 32, 1152], P(('rp', 'pb'))
All inputs are finite; a program needn't handle non-finite values.
Results may differ from a plain program's by a relative error of at most 0.0054.
Values may be sent and summed in bfloat16 or wider, within the bound.
A program may use at most 64 MiB of HBM per device.

v0:
```python
import math

import jax
import jax.numpy as jnp
from jax import lax
from jax.sharding import PartitionSpec as P

NK = 16


def phases(q_rows, r_coords):
    turns = jnp.mod(jnp.sum(q_rows[:, :, None] * r_coords[:, None, :], axis=0), NK)
    angle = turns.astype(jnp.float32) * (2.0 * math.pi / NK)
    cosine = jnp.cos(angle).astype(jnp.bfloat16)
    sine = jnp.sin(angle).astype(jnp.bfloat16)
    return (jnp.concatenate([cosine, -sine], axis=1), jnp.concatenate([sine, cosine], axis=1))


def rotate(fourier, mode_vecs, unit, kq_vecs):
    count = fourier.shape[0]
    bands = kq_vecs.shape[2]
    branches = mode_vecs.shape[2]
    field = fourier.reshape(count, 2, bands, bands, branches)
    e_real, e_imag = (mode_vecs[:, 0], mode_vecs[:, 1])
    e_block = jnp.stack([jnp.stack([e_real, e_imag], 2), jnp.stack([-e_imag, e_real], 2)], 1)
    by_mode = jnp.einsum(
        "qcmnv,qcvdu->qdmnu", field, e_block, preferred_element_type=jnp.float32
    ).astype(jnp.bfloat16)
    u_real, u_imag = (unit[0], unit[1])
    u_block = jnp.stack([jnp.stack([u_real, u_imag], 1), jnp.stack([-u_imag, u_real], 1)], 0)
    by_band = jnp.einsum(
        "qcmnu,cndj->qdmju", by_mode, u_block, preferred_element_type=jnp.float32
    ).astype(jnp.bfloat16)
    v_real, v_imag = (kq_vecs[:, 0], kq_vecs[:, 1])
    v_block = jnp.stack([jnp.stack([v_real, -v_imag], 2), jnp.stack([v_imag, v_real], 2)], 1)
    result = jnp.einsum("qcmju,qcmdi->qdiju", by_band, v_block, preferred_element_type=jnp.float32)
    return result.reshape(count, 2, bands, bands * branches)


def body(wannier_g, rp_coords, q_coords, k_index, k_vectors, kq_vectors, modes):
    q_all = lax.all_gather(q_coords, ("rp", "pb"), axis=1, tiled=True)
    total = q_all.shape[1]
    groups = lax.axis_size("rp")
    block = total // groups
    local = wannier_g.shape[1]
    own_coords = lax.dynamic_slice_in_dim(rp_coords, lax.axis_index("rp") * local, local, 1)
    right = wannier_g.reshape(2 * local, -1)
    left_real, left_imag = phases(q_all, own_coords)
    f_real = jnp.dot(left_real, right, preferred_element_type=jnp.float32)
    f_imag = jnp.dot(left_imag, right, preferred_element_type=jnp.float32)
    summed = lax.psum_scatter(jnp.stack([f_real, f_imag], 1), "rp", scatter_dimension=0, tiled=True)
    fourier = summed.astype(jnp.bfloat16).reshape(block, 2, wannier_g.shape[2], wannier_g.shape[3])
    owned = lax.all_to_all(fourier, "pb", split_axis=0, concat_axis=2, tiled=True)
    select = (jnp.arange(k_vectors.shape[0]) == k_index[0]).astype(jnp.bfloat16)
    unit = jnp.einsum("k,kcnj->cnj", select, k_vectors, preferred_element_type=jnp.float32).astype(
        jnp.bfloat16
    )
    return rotate(owned, modes, unit, kq_vectors)


def solution(mesh):
    return jax.shard_map(
        body,
        mesh=mesh,
        in_specs=(
            P(None, "rp", "pb", None),
            P(),
            P(None, ("rp", "pb")),
            P(),
            P(),
            P(("rp", "pb"), None, None, None),
            P(("rp", "pb"), None, None, None),
        ),
        out_specs=P(("rp", "pb"), None, None, None),
        check_vma=False,
    )
```

profile of v0, /device:TPU:0, one launch (start us, length us, event | category | flops | bytes accessed | tf_op | source)
XLA Modules:
  0.0 110.1 jit_solution(14693091623832037747)
XLA Ops:
  6.5 43.7 %all-gather = s32[32,2,3]{2,1,0:T(2,128)S(1)} all-gather(s32[1,2,3]{2,1,0:T(2,128)} %bitcast.115), channel_id=1, replica_groups=mesh['rp'=2,'pb'=16] {'rp','pb'}, dimensions={0}, use_global_device_ids=true | all-gather | bytes 792 | tf_op jit(solution)/shard_map/all_gather | solution.py:41
  50.3 0.7 constant_dynamic-slice_fusion
  51.0 0.1 multiply_reduce_fusion
  51.1 0.5 fusion.32
  51.6 0.5 cosine_convert_fusion
  52.1 3.2 %copy.104 = bf16[128,8,2,1152]{3,1,2,0:T(8,128)(2,1)S(1)} copy(bf16[128,8,2,1152]{3,2,1,0:T(2,128)(2,1)} %bitcast.107) | data formatting | bytes 9437184
  55.3 0.9 convolution_bitcast_fusion.1
  56.2 0.9 convolution_bitcast_fusion
  57.2 1.1 pad_maximum_fusion
  59.1 0.2 fusion.15
  59.6 17.1 %reduce-scatter.2.cloned.1.call-done = f32[32,2,2304]{2,0,1:T(8,128)} async-done(((f32[64,2,2304]{2,0,1:T(8,128)}), f32[32,2,2304]{2,0,1:T(8,128)}) %reduce-scatter.2.cloned.1.call-update) | async-done | bytes 589840 | tf_op jit(solution)/shard_map/reduce_scatter | solution.py:51
  76.7 1.1 convert_element_type.32
  77.8 0.9 copy.77
  78.7 5.6 %all-to-all-start = ((bf16[32,2,2,1152]{3,2,1,0:T(2,128)(2,1)}), bf16[32,2,2,1152]{3,2,1,0:T(2,128)(2,1)S(1)}, u32[]{:S(2)}, u32[]{:S(2)}) async-start(bf16[32,2,2,1152]{3,2,1,0:T(2,128)(2,1)} %copy.77), calls=%async_computation.1 | async-start | bytes 589824 | tf_op jit(solution)/shard_map/all_to_all | solution.py:53
  84.4 0.1 maximum_bitcast_fusion.3
  84.5 0.1 maximum_bitcast_fusion
  84.7 10.2 %all-to-all-done = bf16[32,2,2,1152]{3,2,1,0:T(2,128)(2,1)S(1)} async-done(((bf16[32,2,2,1152]{3,2,1,0:T(2,128)(2,1)}), bf16[32,2,2,1152]{3,2,1,0:T(2,128)(2,1)S(1)}, u32[]{:S(2)}, u32[]{:S(2)}) %all-to-all-start) | async-done | bytes 294944 | tf_op jit(solution)/shard_map/all_to_all | solution.py:53
  94.9 0.2 copy.97
  95.1 3.0 %reshape.54 = bf16[2,2,32,32,36,1]{4,3,1,2,0,5:T(8,128)(2,1)S(1)} reshape(bf16[2,2,16,2,1152]{4,1,3,2,0:T(2,128)(2,1)S(1)} %copy.97) | data formatting | bytes 589824 | tf_op jit(solution)/shard_map/reshape | solution.py:23
  98.1 0.5 fusion
  98.6 0.5 fusion.1
  99.1 0.5 convolution_bitcast_fusion.2
  99.6 1.2 %copy.83 = f32[2,2,32,32,36]{4,3,2,1,0:T(8,128)S(1)} copy(f32[2,2,32,32,36]{4,2,3,1,0:T(8,128)S(1)} %convolution_bitcast_fusion.2) | data formatting | bytes 1179648 | tf_op jit(solution)/shard_map/qcmju,qcmdi->qdiju/dot_general | solution.py:36
  100.8 2.4 %reshape.48 = f32[2,2,32,1152]{3,2,1,0:T(8,128)} reshape(f32[2,2,32,32,36]{4,3,2,1,0:T(8,128)S(1)} %copy.83) | data formatting | bytes 1179648 | tf_op jit(solution)/shard_map/reshape | solution.py:37
  (22 shorter events, 0.6 us)
Async XLA Ops:
  6.5 52.5 %copy-start = (bf16[8,2,32,32]{3,2,1,0:T(8,128)(2,1)S(1)}, bf16[8,2,32,32]{3,2,1,0:T(8,128)(2,1)}, u32[]{:S(2)}) copy-start(bf16[8,2,32,32]{3,2,1,0:T(8,128)(2,1)} %param.11) | copy-start | bytes 98308
  6.5 70.1 %reduce-scatter.2.cloned.1.call-start = ((), (), s32[]{:S(2)}) async-start(), calls=%async_computation.2 | async-start | bytes 1769472 | tf_op jit(solution)/shard_map/reduce_scatter | solution.py:51
  57.1 1.1 %copy-start.1 = (bf16[2,2,36,36]{3,1,2,0:T(2,128)(2,1)S(1)}, bf16[2,2,36,36]{3,1,2,0:T(2,128)(2,1)}, u32[]{:S(2)}) copy-start(bf16[2,2,36,36]{3,1,2,0:T(2,128)(2,1)} %param.13) | copy-start | bytes 31108
  57.2 2.2 %copy-start.2 = (bf16[2,2,32,32]{3,2,1,0:T(8,128)(2,1)S(1)}, bf16[2,2,32,32]{3,2,1,0:T(8,128)(2,1)}, u32[]{:S(2)}) copy-start(bf16[2,2,32,32]{3,2,1,0:T(8,128)(2,1)} %param.12) | copy-start | bytes 24580
  78.7 16.2 %all-to-all-start = ((bf16[32,2,2,1152]{3,2,1,0:T(2,128)(2,1)}), bf16[32,2,2,1152]{3,2,1,0:T(2,128)(2,1)S(1)}, u32[]{:S(2)}, u32[]{:S(2)}) async-start(bf16[32,2,2,1152]{3,2,1,0:T(2,128)(2,1)} %copy.77), calls=%async_computation.1 | async-start | bytes 589824 | tf_op jit(solution)/shard_map/all_to_all | solution.py:53
Sparse Core Ops, SparseCore 0:
  58.4 18.1 reduce-scatter.1
where the time goes:
time: 110 us
  blocking collectives  43.7 us (40%)
  waiting for transfers between devices  27.3 us (25%)
  between operations  14.3 us (13%)
  local copies, waits for them, and re-layouts  12.2 us (11%)
  starting transfers between devices  5.61 us (5%)
  other arithmetic  3.58 us (3%)
  matrix products  3.51 us (3%)
    all_gather x1, blocking collectives, body(): q_all = lax.all_gather(q_coords, ('rp', 'pb'), axis=1, tiled=True)  43.7 us
    reduce_scatter x1, waiting for transfers between devices, body(): lax.psum_scatter(jnp.stack([f_real, f_imag], 1), 'rp', scatter_dimension=...  17.1 us
    all_to_all x1, waiting for transfers between devices, body(): lax.all_to_all(fourier, 'pb', split_axis=0, concat_axis=2, tiled=True)  10.2 us
    all_to_all x1, starting transfers between devices, body(): lax.all_to_all(fourier, 'pb', split_axis=0, concat_axis=2, tiled=True)  5.61 us
    unnamed x11, local copies, waits for them, and re-layouts  3.46 us
    reshape x2, local copies, waits for them, and re-layouts, rotate(): field = fourier.reshape(count, 2, bands, bands, branches)  3.2 us
    reshape x1, local copies, waits for them, and re-layouts, rotate(): return result.reshape(count, 2, bands, bands * branches)  2.44 us
  transfers between devices with their start and end apart: 2, of which 2 were waited for; matrix products, arithmetic and copies ran while one was open for 1% of the time, Pallas kernels for 0%

commit v1 on v0

v1 whole, which is shorter than its diff:
```python
import functools

import jax
import jax.numpy as jnp
import numpy as np
from jax import lax
from jax.experimental import pallas as pl
from jax.experimental.pallas import tpu as pltpu
from jax.sharding import PartitionSpec as P

NK = 16
LANES = 128
MESH = pl.DeviceIdType.MESH
F32 = jnp.float32
BF16 = jnp.bfloat16
ODD = np.linalg.solve(
    np.array([[h, h**3, h**5, h**7] for h in (1.0, 2.0, 3.0, 4.0)]),
    np.sin(np.pi * np.arange(1, 5) / 8.0),
)


def dot(a, b, dims=((1,), (0,))):
    return lax.dot_general(a, b, (dims, ((), ())), preferred_element_type=F32)


def iota(shape, axis):
    return lax.broadcasted_iota(jnp.int32, shape, axis)


def picks(rows, cols, hit):
    return jnp.where(hit(iota((rows, cols), 0), iota((rows, cols), 1)), 1.0, 0.0).astype(BF16)


def wave(turns):
    h = (jnp.abs((turns & (NK - 1)) - NK // 2) - NK // 4).astype(F32)
    s = h * h
    return h * (ODD[0] + s * (ODD[1] + s * (ODD[2] + s * ODD[3])))


def kernel(
    cfg, g_hbm, rp_ref, q_ref, k_ref, kv_ref, v_ref, e_ref, o_ref,
    g_buf, qrow, q_all, send, recv, w_buf, rmat, g_sem, qs_sem, qr_sem, s_sem, r_sem,
):
    n_rp, n_pb, qd, local, M, cols, bands, nu, RB, paired = cfg
    n = n_rp * n_pb
    ip, ib = lax.axis_index("rp"), lax.axis_index("pb")
    me = ip * n_pb + ib
    depth = local * M

    def place(k):
        peer = lax.rem(me + k, n)
        return peer, (lax.div(peer, n_pb), lax.rem(peer, n_pb))

    barrier = pltpu.get_barrier_semaphore()

    def greet(k, c):
        pl.semaphore_signal(barrier, inc=1, device_id=place(k)[1], device_id_type=MESH)
        return c

    lax.fori_loop(1, n, greet, 0)

    tiles = cols // LANES
    loads = []
    for t in range(tiles):
        lanes = pl.ds(LANES * t, LANES)
        src = g_hbm.at[:, :, :, lanes] if paired else g_hbm.at[:, lanes]
        loads.append(pltpu.make_async_copy(src, g_buf.at[t], g_sem.at[t]))
    for c in loads:
        c.start()

    lane = iota((1, LANES), 1)
    row = jnp.zeros((1, LANES), jnp.int32)
    for d in range(3):
        for j in range(qd):
            row = jnp.where(lane == d * qd + j, q_ref[d, j], row)
    qrow[...] = (row & (NK - 1)).astype(F32)

    pl.semaphore_wait(barrier, n - 1)

    def q_copy(k):
        peer, to = place(k)
        return pltpu.make_async_remote_copy(
            src_ref=qrow, dst_ref=q_all.at[me], send_sem=qs_sem.at[peer],
            recv_sem=qr_sem.at[me], device_id=to, device_id_type=MESH,
        )

    def q_start(k, c):
        q_copy(k).start()
        return c

    lax.fori_loop(1, n, q_start, 0)
    q_all[me] = qrow[...]

    own = rp_ref[:, pl.ds(pl.multiple_of(ip * local, LANES), local)] & (NK - 1)
    spread = picks(local, depth, lambda a, b: a == b // M)
    own = dot(own.astype(F32).astype(BF16), spread)
    which = iota((LANES, depth), 0) // qd
    big = jnp.zeros((LANES, depth), F32)
    for d in range(3):
        big = jnp.where(which == d, own[d : d + 1, :], big)
    rmat[...] = big.astype(BF16)

    def q_wait(k, c):
        peer, to = place(k)
        arrived = pltpu.make_async_remote_copy(
            src_ref=qrow, dst_ref=q_all.at[peer], send_sem=qs_sem.at[peer],
            recv_sem=qr_sem.at[peer], device_id=to, device_id_type=MESH,
        )
        arrived.wait_recv()
        q_copy(k).wait_send()
        return c

    lax.fori_loop(1, n, q_wait, 0)

    rows = n * RB
    coords = jnp.broadcast_to(q_all[...], (n, RB, LANES)).reshape(rows, LANES)
    slot = iota((rows, LANES), 0) % RB
    coords = jnp.where(iota((rows, LANES), 1) % qd == slot // (2 * M), coords, 0.0)
    turns = dot(coords.astype(BF16), rmat[...]).astype(jnp.int32)
    slot = iota((rows, 1), 0) % RB
    part = (slot // M) % 2
    keep = (slot % M) == (iota((1, depth), 1) % M)
    left = []
    for shift in (jnp.where(part == 1, 3 * NK // 4, 0), jnp.where(part == 1, 0, NK // 4)):
        left.append(jnp.where(keep, wave(turns + shift), 0.0).astype(BF16))
    left = jnp.concatenate(left, axis=1)

    for t in range(0, tiles, 2):
        parts = []
        for u in range(t, min(t + 2, tiles)):
            loads[u].wait()
            parts.append(g_buf.at[u].reshape(2 * depth, LANES)[...] if paired else g_buf[u])
        right = parts[0] if len(parts) == 1 else jnp.concatenate(parts, axis=1)
        f = dot(left, right).astype(BF16)
        send[:, :, LANES * t : LANES * (t + len(parts))] = f.reshape(n, RB, LANES * len(parts))

    def f_copy(k):
        peer, to = place(k)
        return pltpu.make_async_remote_copy(
            src_ref=send.at[peer], dst_ref=recv.at[me], send_sem=s_sem.at[peer],
            recv_sem=r_sem.at[me], device_id=to, device_id_type=MESH,
        )

    def f_start(k, c):
        f_copy(k).start()
        return c

    lax.fori_loop(1, n, f_start, 0)
    recv[me] = send[me]

    unit = kv_ref[k_ref[0]]
    of_band_t = picks(bands, cols, lambda b, a: (a >= nu * b) & (a < nu * b + nu))
    of_mode_t = picks(nu, cols, lambda b, a: (a - b + nu * bands) % nu == 0)
    u_right = [dot(unit[c], of_band_t).astype(BF16) for c in range(2)]
    e_right = [[dot(e_ref[q, c], of_mode_t).astype(BF16) for c in range(2)] for q in range(qd)]
    for t in range(tiles):
        first = t * LANES
        of_band = picks(LANES, bands, lambda a, b: (a + first >= nu * b) & (a + first < nu * b + nu))
        of_mode = picks(LANES, nu, lambda a, b: (a + first - b + nu * bands) % nu == 0)
        ur, ui = [dot(of_band, m) for m in u_right]
        for q in range(qd):
            er, ei = [dot(of_mode, m) for m in e_right[q]]
            w_buf[q, 0, first : first + LANES, :] = (ur * er - ui * ei).astype(BF16)
            w_buf[q, 1, first : first + LANES, :] = (ur * ei + ui * er).astype(BF16)

    col = iota((bands, rows), 1)
    slot = col % RB
    m_of = ((col // RB) % n_pb) * M + slot % M
    pick_m = jnp.where(iota((bands, rows), 0) == m_of, 1.0, 0.0).astype(BF16)
    real_in = (slot // M) % 2 == 0
    blocks = []
    for q in range(qd):
        a_r, a_i = [dot(v_ref[q, c], pick_m, ((0,), (0,))) for c in range(2)]
        mine = slot // (2 * M) == q
        blocks.append(jnp.where(mine, jnp.where(real_in, a_r, a_i), 0.0))
        blocks.append(jnp.where(mine, jnp.where(real_in, -a_i, a_r), 0.0))
    v_left = jnp.concatenate(blocks, axis=0).astype(BF16)

    def f_wait(k, c):
        peer, to = place(k)
        pltpu.make_async_remote_copy(
            src_ref=send.at[peer], dst_ref=recv.at[peer], send_sem=s_sem.at[peer],
            recv_sem=r_sem.at[peer], device_id=to, device_id_type=MESH,
        ).wait_recv()
        f_copy(k).wait_send()
        return c

    lax.fori_loop(1, n, f_wait, 0)

    y = dot(v_left, recv[...].reshape(rows, cols)).astype(BF16)
    for q in range(qd):
        yq = y[2 * bands * q : 2 * bands * (q + 1)]
        a = dot(yq, w_buf[q, 0])
        b = dot(yq, w_buf[q, 1])
        o_ref[q, 0] = a[:bands] - b[bands:]
        o_ref[q, 1] = a[bands:] + b[:bands]


def body(wannier_g, rp_coords, q_coords, k_index, k_vectors, kq_vectors, modes):
    n_rp, n_pb = lax.axis_size("rp"), lax.axis_size("pb")
    n = n_rp * n_pb
    qd = q_coords.shape[1]
    _, local, M, cols = wannier_g.shape
    bands, nu = kq_vectors.shape[2], modes.shape[2]
    RB = -(-(qd * 2 * M) // 8) * 8
    paired = M == 2
    tiles = cols // LANES
    right = wannier_g if paired else wannier_g.reshape(2 * local * M, cols)
    g_shape = (tiles, 2, local, M, LANES) if paired else (tiles, 2 * local * M, LANES)
    cfg = (n_rp, n_pb, qd, local, M, cols, bands, nu, RB, paired)
    vmem = pl.BlockSpec(memory_space=pltpu.VMEM)
    smem = pl.BlockSpec(memory_space=pltpu.SMEM)
    return pl.pallas_call(
        functools.partial(kernel, cfg),
        out_shape=jax.ShapeDtypeStruct((qd, 2, bands, cols), F32),
        in_specs=[pl.BlockSpec(memory_space=pl.ANY), vmem, smem, smem, vmem, vmem, vmem],
        out_specs=vmem,
        scratch_shapes=[
            pltpu.VMEM(g_shape, BF16),
            pltpu.VMEM((1, LANES), F32),
            pltpu.VMEM((n, 1, LANES), F32),
            pltpu.VMEM((n, RB, cols), BF16),
            pltpu.VMEM((n, RB, cols), BF16),
            pltpu.VMEM((qd, 2, cols, cols), BF16),
            pltpu.VMEM((LANES, local * M), BF16),
            pltpu.SemaphoreType.DMA((tiles,)),
            pltpu.SemaphoreType.DMA((n,)),
            pltpu.SemaphoreType.DMA((n,)),
            pltpu.SemaphoreType.DMA((n,)),
            pltpu.SemaphoreType.DMA((n,)),
        ],
        compiler_params=pltpu.CompilerParams(
            collective_id=0, has_side_effects=True, vmem_limit_bytes=60 * 2**20
        ),
    )(right, rp_coords, q_coords, k_index, k_vectors, kq_vectors, modes)


def solution(mesh):
    return jax.shard_map(
        body,
        mesh=mesh,
        in_specs=(
            P(None, "rp", "pb", None),
            P(),
            P(None, ("rp", "pb")),
            P(),
            P(),
            P(("rp", "pb"), None, None, None),
            P(("rp", "pb"), None, None, None),
        ),
        out_specs=P(("rp", "pb"), None, None, None),
        check_vma=False,
    )
```

time: 110 us -> 40.8 us (0.37)
  blocking collectives: 43.7 us -> 0 us
  Pallas kernels: 0 us -> 35.2 us
  waiting for transfers between devices: 27.3 us -> 0 us
  between operations: 14.3 us -> 0.66 us
  local copies, waits for them, and re-layouts: 12.2 us -> 4.66 us
  starting transfers between devices: 5.61 us -> 0 us
  other arithmetic: 3.58 us -> 0 us
  matrix products: 3.51 us -> 0 us
    all_gather x1 -> x0, blocking collectives: 43.7 us -> none  [body(): q_all = lax.all_gather(q_coords, ('rp', 'pb'), axis=1, tiled=True)]
    pallas_call x0 -> x1, Pallas kernels: none -> 35.2 us  [body(): pl.pallas_call(functools.partial(kernel, cfg), out_shape=jax.ShapeDtypeSt...]
    reduce_scatter x1 -> x0, waiting for transfers between devices: 17.1 us -> none  [body(): lax.psum_scatter(jnp.stack([f_real, f_imag], 1), 'rp', scatter_dimension=...]
    all_to_all x1 -> x0, waiting for transfers between devices: 10.2 us -> none  [body(): lax.all_to_all(fourier, 'pb', split_axis=0, concat_axis=2, tiled=True)]
    reshape x5 -> x0, local copies, waits for them, and re-layouts: 6.63 us -> none  [the longest x2 3.2 us: rotate(): field = fourier.reshape(count, 2, bands, bands, branches)]
    all_to_all x1 -> x0, starting transfers between devices: 5.61 us -> none  [body(): lax.all_to_all(fourier, 'pb', split_axis=0, concat_axis=2, tiled=True)]
    dot_general x6 -> x0, matrix products: 3.51 us -> none  [the longest x1 0.93 us: body(): f_real = jnp.dot(left_real, right, preferred_element_type=jnp.float32)]
    convert_element_type x2 -> x0, other arithmetic: 1.58 us -> none  [the longest x1 1.1 us: body(): summed.astype(jnp.bfloat16)]
  transfers between devices with their start and end apart: 2 -> 0, of which waited for: 2 -> 0; matrix products, arithmetic and copies ran while one was open for 1% -> 0% of each run, Pallas kernels for 0% -> 0%
where the time goes in v1:
time: 40.8 us; the launch traced here: 40.6 us
  Pallas kernels  35.2 us (86%)
  local copies, waits for them, and re-layouts  4.66 us (11%)
  between operations  0.66 us (2%)
    pallas_call x1, Pallas kernels, body(): pl.pallas_call(functools.partial(kernel, cfg), out_shape=jax.ShapeDtypeSt...  35.2 us
    unnamed x3, local copies, waits for them, and re-layouts  4.66 us

profile of v1, /device:TPU:0, one launch (start us, length us, event | category | flops | bytes accessed | tf_op | source)
XLA Modules:
  0.0 40.6 jit_solution(5183556353423126586)
XLA Ops:
  0.7 1.4 %copy.8.q_ref = s32[3,2]{1,0:T(4,128)} copy(s32[3,2]{0,1:T(2,128)} %param.9) | data formatting | bytes 48 | tf_op args[2]
  2.0 1.4 %copy.9.e_ref = bf16[2,2,36,36]{3,2,1,0:T(8,128)(2,1)} copy(bf16[2,2,36,36]{3,1,2,0:T(2,128)(2,1)} %param.13) | data formatting | bytes 20736 | tf_op args[6]
  3.4 35.2 %shard_map.73 = f32[2,2,32,1152]{3,2,1,0:T(8,128)} custom-call(bf16[2,512,2,1152]{3,2,1,0:T(2,128)(2,1)} %g_hbm.1, s32[3,1024]{1,0:T(4,128)} %rp_ref.1, s32[3,2]{1,0:T(4,128)} %copy.8.q_ref, s32[1]{0:T(128)S(6)} %copy.11.k_ref, bf16[8,2,32,32]{3,2,1,0:T(8,128)(2,1)} %kv_ref.1, bf16[2,2,32,32]{3,2,1,0:T(8,128)(2,1)} %v_ref.1, bf16[2,2,36,36]{3,2,1,0:T(8,128)(2,1)} %copy.9.e_ref), custom_call_target="tpu_custom_call" | custom-call | tf_op jit(solution)/shard_map/pallas_call | solution.py:213
  38.6 1.9 %copy.12 = f32[2,2,32,1152]{3,2,1,0:T(8,128)} copy(f32[2,2,32,1152]{3,2,1,0:T(8,128)} %shard_map.73) | data formatting | bytes 1179648

commit v2 on v1

v2 whole, which is shorter than its diff:
```python
import functools

import jax
import jax.numpy as jnp
import numpy as np
from jax import lax
from jax.experimental import pallas as pl
from jax.experimental.pallas import tpu as pltpu
from jax.sharding import PartitionSpec as P

NK = 16
LANES = 128
MESH = pl.DeviceIdType.MESH
F32 = jnp.float32
BF16 = jnp.bfloat16
ODD = np.linalg.solve(
    np.array([[h, h**3, h**5, h**7] for h in (1.0, 2.0, 3.0, 4.0)]),
    np.sin(np.pi * np.arange(1, 5) / 8.0),
)


def dot(a, b, dims=((1,), (0,))):
    return lax.dot_general(a, b, (dims, ((), ())), preferred_element_type=F32)


def iota(shape, axis):
    return lax.broadcasted_iota(jnp.int32, shape, axis)


def picks(rows, cols, hit):
    return jnp.where(hit(iota((rows, cols), 0), iota((rows, cols), 1)), 1.0, 0.0).astype(BF16)


def wave(sixteenths):
    h = NK // 4 - NK * jnp.abs(sixteenths - jnp.floor(sixteenths + 0.5))
    s = h * h
    return h * (ODD[0] + s * (ODD[1] + s * (ODD[2] + s * ODD[3])))


def wrapped(a, b, size):
    c = a + b
    return jnp.where(c >= size, c - size, c)


def cuts(tiles):
    if tiles < 8:
        return [tiles]
    first, rest = 2, tiles - 2
    sizes = [first] + [rest // 3 + (k < rest % 3) for k in range(3)]
    return sizes


def kernel(
    cfg, g_hbm, rp_hbm, q_ref, k_ref, kv_hbm, v_hbm, e_hbm, o_ref,
    g_buf, rp_ref, kv_ref, v_ref, e_ref, qrow, q_all, xsend, xrecv, red, recv, w_buf, rmat, v_left,
    g_sem, in_sem, qs_sem, qr_sem, xs_sem, xr_sem, s_sem, r_sem,
):
    n_rp, n_pb, qd, local, M, cols, bands, nu, RB, paired = cfg
    n = n_rp * n_pb
    ip, ib = lax.axis_index("rp"), lax.axis_index("pb")
    me = ip * n_pb + ib
    depth = local * M
    half = n_pb * RB
    tiles = cols // LANES

    def to_all(act):
        for dp in range(n_rp):
            p = wrapped(ip, dp, n_rp)

            def one(db, c, p=p):
                act(p, wrapped(ib, db, n_pb))
                return c

            lax.fori_loop(1 if dp == 0 else 0, n_pb, one, 0)

    barrier = pltpu.get_barrier_semaphore()
    to_all(
        lambda p, b: pl.semaphore_signal(barrier, inc=1, device_id=(p, b), device_id_type=MESH)
    )

    inputs = [
        pltpu.make_async_copy(a, b, in_sem.at[k])
        for k, (a, b) in enumerate(
            ((rp_hbm, rp_ref), (kv_hbm, kv_ref), (v_hbm, v_ref), (e_hbm, e_ref))
        )
    ]
    for c in inputs:
        c.start()
    loads = []
    for t in range(tiles):
        lanes = pl.ds(LANES * t, LANES)
        src = g_hbm.at[:, :, :, lanes] if paired else g_hbm.at[:, lanes]
        loads.append(pltpu.make_async_copy(src, g_buf.at[t], g_sem.at[t]))
    for c in loads:
        c.start()

    lane = iota((1, LANES), 1)
    row = jnp.zeros((1, LANES), jnp.int32)
    for d in range(3):
        for j in range(qd):
            row = jnp.where(lane == d * qd + j, q_ref[j, d], row)
    qrow[...] = (row & (NK - 1)).astype(F32)
    q_all[me] = qrow[...]
    for c in inputs:
        c.wait()

    own = rp_ref[:, pl.ds(pl.multiple_of(ip * local, LANES), local)] & (NK - 1)
    spread = picks(local, depth, lambda a, b: a == b // M)
    own = dot((own.astype(F32) * (1.0 / NK)).astype(BF16), spread)
    which = iota((LANES, depth), 0) // qd
    big = jnp.zeros((LANES, depth), F32)
    for d in range(3):
        big = jnp.where(which == d, own[d : d + 1, :], big)
    rmat[...] = big.astype(BF16)

    slot = iota((bands, half), 1) % RB
    m_of = (iota((bands, half), 1) // RB) * M + slot % M
    pick_m = jnp.where(iota((bands, half), 0) == m_of, 1.0, 0.0).astype(BF16)
    real_in = (slot // M) % 2 == 0
    for q in range(qd):
        a_r, a_i = [dot(v_ref[q, c], pick_m, ((0,), (0,))) for c in range(2)]
        mine = slot // (2 * M) == q
        top = jnp.where(mine, jnp.where(real_in, a_r, a_i), 0.0)
        low = jnp.where(mine, jnp.where(real_in, -a_i, a_r), 0.0)
        v_left[2 * bands * q : 2 * bands * (q + 1), :] = jnp.concatenate([top, low], 0).astype(BF16)

    unit = kv_ref[k_ref[0]]
    of_band_t = picks(bands, cols, lambda b, a: (a >= nu * b) & (a < nu * b + nu))
    of_mode_t = picks(nu, cols, lambda b, a: (a - b + nu * bands) % nu == 0)
    u_right = [dot(unit[c], of_band_t).astype(BF16) for c in range(2)]
    e_right = [[dot(e_ref[q, :, c, :], of_mode_t).astype(BF16) for c in range(2)] for q in range(qd)]

    def combine(t):
        first = t * LANES
        of_band = picks(LANES, bands, lambda a, b: (a + first >= nu * b) & (a + first < nu * b + nu))
        of_mode = picks(LANES, nu, lambda a, b: (a + first - b + nu * bands) % nu == 0)
        ur, ui = [dot(of_band, m) for m in u_right]
        for q in range(qd):
            er, ei = [dot(of_mode, m) for m in e_right[q]]
            w_buf[q, 0, first : first + LANES, :] = (ur * er - ui * ei).astype(BF16)
            w_buf[q, 1, first : first + LANES, :] = (ur * ei + ui * er).astype(BF16)

    early = tiles // 2
    for t in range(early):
        combine(t)

    pl.semaphore_wait(barrier, n - 1)

    def q_copy(p, b, slot_of):
        return pltpu.make_async_remote_copy(
            src_ref=qrow, dst_ref=q_all.at[slot_of], send_sem=qs_sem.at[p * n_pb + b],
            recv_sem=qr_sem.at[slot_of], device_id=(p, b), device_id_type=MESH,
        )

    to_all(lambda p, b: q_copy(p, b, me).start())

    def q_done(p, b):
        q_copy(p, b, p * n_pb + b).wait_recv()
        q_copy(p, b, me).wait_send()

    to_all(q_done)

    coords = jnp.concatenate(
        [
            jnp.broadcast_to(q_all[pl.ds(wrapped(ip, dp, n_rp) * n_pb, n_pb)], (n_pb, RB, LANES))
            for dp in range(n_rp)
        ],
        axis=0,
    ).reshape(n * RB, LANES)
    slot = iota((n * RB, LANES), 0) % RB
    coords = jnp.where(iota((n * RB, LANES), 1) % qd == slot // (2 * M), coords, 0.0)
    turns = dot(coords.astype(BF16), rmat[...])
    slot = iota((n * RB, 1), 0) % RB
    imag = (slot // M) % 2 == 1
    keep = (slot % M) == (iota((1, depth), 1) % M)
    left = jnp.concatenate(
        [
            jnp.where(keep, wave(turns + shift), 0.0).astype(BF16)
            for shift in (jnp.where(imag, 0.75, 0.0), jnp.where(imag, 0.0, 0.25))
        ],
        axis=1,
    )

    sizes = cuts(tiles)
    firsts = [sum(sizes[:c]) for c in range(len(sizes))]
    lanes = [slice(LANES * a, LANES * (a + b)) for a, b in zip(firsts, sizes)]

    def x_copy(dp, c):
        part = (slice(None), slice(None), lanes[c])
        return pltpu.make_async_remote_copy(
            src_ref=xsend.at[(dp - 1, *part)], dst_ref=xrecv.at[(dp - 1, *part)],
            send_sem=xs_sem.at[dp - 1, c], recv_sem=xr_sem.at[dp - 1, c],
            device_id=(wrapped(ip, dp, n_rp), ib), device_id_type=MESH,
        )

    def f_copy(b, block, c):
        return pltpu.make_async_remote_copy(
            src_ref=red.at[b, :, lanes[c]], dst_ref=recv.at[block, :, lanes[c]],
            send_sem=s_sem.at[c, b], recv_sem=r_sem.at[c, block],
            device_id=(ip, b), device_id_type=MESH,
        )

    def to_group(act):
        def one(db, c):
            act(wrapped(ib, db, n_pb))
            return c

        lax.fori_loop(1, n_pb, one, 0)

    owned = {}

    def fourier(c):
        parts = []
        for u in range(firsts[c], firsts[c] + sizes[c]):
            loads[u].wait()
            parts.append(g_buf.at[u].reshape(2 * depth, LANES)[...] if paired else g_buf[u])
        right = parts[0] if len(parts) == 1 else jnp.concatenate(parts, axis=1)
        f = dot(left, right)
        owned[c] = f[:half]
        wide = LANES * sizes[c]
        for dp in range(1, n_rp):
            away = f[dp * half : (dp + 1) * half].astype(BF16)
            xsend[dp - 1, :, :, lanes[c]] = away.reshape(n_pb, RB, wide)
            x_copy(dp, c).start()

    def reduce(c):
        total = owned.pop(c)
        wide = LANES * sizes[c]
        for dp in range(1, n_rp):
            x_copy(dp, c).wait()
            total = total + xrecv[dp - 1, :, :, lanes[c]].astype(F32).reshape(half, wide)
        red[:, :, lanes[c]] = total.astype(BF16).reshape(n_pb, RB, wide)
        to_group(lambda b: f_copy(b, ib, c).start())
        recv[ib, :, lanes[c]] = red[ib, :, lanes[c]]

    count = len(sizes)
    fourier(0)
    for c in range(1, count):
        fourier(c)
        if c >= 2:
            reduce(c - 2)
    for c in range(max(count - 2, 0), count):
        reduce(c)
    for t in range(early, tiles):
        combine(t)

    sums = [[0.0, 0.0] for _ in range(qd)]
    for c in range(count):

        def f_done(b, c=c):
            f_copy(b, b, c).wait_recv()
            f_copy(b, ib, c).wait_send()

        to_group(f_done)
        block = recv[:, :, lanes[c]].reshape(half, LANES * sizes[c])
        y = dot(v_left[...], block).astype(BF16)
        for q in range(qd):
            yq = y[2 * bands * q : 2 * bands * (q + 1)]
            for part in range(2):
                sums[q][part] = sums[q][part] + dot(yq, w_buf[q, part, lanes[c], :])
    for q in range(qd):
        a, b = sums[q]
        o_ref[q, 0] = a[:bands] - b[bands:]
        o_ref[q, 1] = a[bands:] + b[:bands]


def body(wannier_g, rp_coords, q_coords, k_index, k_vectors, kq_vectors, modes):
    n_rp, n_pb = lax.axis_size("rp"), lax.axis_size("pb")
    n = n_rp * n_pb
    qd = q_coords.shape[1]
    _, local, M, cols = wannier_g.shape
    bands, nu = kq_vectors.shape[2], modes.shape[2]
    RB = -(-(qd * 2 * M) // 8) * 8
    paired = M == 2
    tiles = cols // LANES
    chunks = len(cuts(tiles))
    right = wannier_g if paired else wannier_g.reshape(2 * local * M, cols)
    g_shape = (tiles, 2, local, M, LANES) if paired else (tiles, 2 * local * M, LANES)
    cfg = (n_rp, n_pb, qd, local, M, cols, bands, nu, RB, paired)
    hbm = pl.BlockSpec(memory_space=pltpu.HBM)
    smem = pl.BlockSpec(memory_space=pltpu.SMEM)
    modes = modes.transpose(0, 2, 1, 3)
    others = max(n_rp - 1, 1)
    return pl.pallas_call(
        functools.partial(kernel, cfg),
        out_shape=jax.ShapeDtypeStruct((qd, 2, bands, cols), F32),
        in_specs=[hbm, hbm, smem, smem, hbm, hbm, hbm],
        out_specs=pl.BlockSpec(memory_space=pltpu.VMEM),
        scratch_shapes=[
            pltpu.VMEM(g_shape, BF16),
            pltpu.VMEM(rp_coords.shape, jnp.int32),
            pltpu.VMEM(k_vectors.shape, BF16),
            pltpu.VMEM(kq_vectors.shape, BF16),
            pltpu.VMEM(modes.shape, BF16),
            pltpu.VMEM((1, LANES), F32),
            pltpu.VMEM((n, 1, LANES), F32),
            pltpu.VMEM((others, n_pb, RB, cols), BF16),
            pltpu.VMEM((others, n_pb, RB, cols), BF16),
            pltpu.VMEM((n_pb, RB, cols), BF16),
            pltpu.VMEM((n_pb, RB, cols), BF16),
            pltpu.VMEM((qd, 2, cols, cols), BF16),
            pltpu.VMEM((LANES, local * M), BF16),
            pltpu.VMEM((qd * 2 * bands, n_pb * RB), BF16),
            pltpu.SemaphoreType.DMA((tiles,)),
            pltpu.SemaphoreType.DMA((4,)),
            pltpu.SemaphoreType.DMA((n,)),
            pltpu.SemaphoreType.DMA((n,)),
            pltpu.SemaphoreType.DMA((others, chunks)),
            pltpu.SemaphoreType.DMA((others, chunks)),
            pltpu.SemaphoreType.DMA((chunks, n_pb)),
            pltpu.SemaphoreType.DMA((chunks, n_pb)),
        ],
        compiler_params=pltpu.CompilerParams(
            collective_id=0, has_side_effects=True, vmem_limit_bytes=60 * 2**20
        ),
    )(right, rp_coords, q_coords.T, k_index, k_vectors, kq_vectors, modes)


def solution(mesh):
    return jax.shard_map(
        body,
        mesh=mesh,
        in_specs=(
            P(None, "rp", "pb", None),
            P(),
            P(None, ("rp", "pb")),
            P(),
            P(),
            P(("rp", "pb"), None, None, None),
            P(("rp", "pb"), None, None, None),
        ),
        out_specs=P(("rp", "pb"), None, None, None),
        check_vma=False,
    )
```

time: 40.8 us -> 36.8 us (0.902)
  local copies, waits for them, and re-layouts: 4.66 us -> 1.92 us
  Pallas kernels: 35.2 us -> 34 us
    unnamed x3 -> x1, local copies, waits for them, and re-layouts: 4.66 us -> 1.92 us
    pallas_call x1, Pallas kernels: 35.2 us -> 34 us  [body(): pl.pallas_call(functools.partial(kernel, cfg), out_shape=jax.ShapeDtypeSt...]
where the time goes in v2:
time: 36.8 us; the launch traced here: 36.6 us
  Pallas kernels  34 us (92%)
  local copies, waits for them, and re-layouts  1.92 us (5%)
  between operations  0.66 us (2%)
    pallas_call x1, Pallas kernels, body(): pl.pallas_call(functools.partial(kernel, cfg), out_shape=jax.ShapeDtypeSt...  34 us
    unnamed x1, local copies, waits for them, and re-layouts  1.92 us

profile of v2, /device:TPU:0, one launch (start us, length us, event | category | flops | bytes accessed | tf_op | source)
XLA Modules:
  0.0 36.6 jit_solution(15845684237527283976)
XLA Ops:
  0.7 34.0 %shard_map.73 = f32[2,2,32,1152]{3,2,1,0:T(8,128)} custom-call(bf16[2,512,2,1152]{3,2,1,0:T(2,128)(2,1)} %g_hbm.1, s32[3,1024]{1,0:T(4,128)} %rp_hbm.1, s32[2,3]{1,0:T(2,128)} %bitcast.3, s32[1]{0:T(128)S(6)} %copy.9.k_ref, bf16[8,2,32,32]{3,2,1,0:T(8,128)(2,1)} %kv_hbm.1, bf16[2,2,32,32]{3,2,1,0:T(8,128)(2,1)} %v_hbm.1, bf16[2,36,2,36]{3,2,1,0:T(2,128)(2,1)} %bitcast.2), custom_call_target="tpu_custom_call" | custom-call | tf_op jit(solution)/shard_map/pallas_call | solution.py:284
  34.7 1.9 %copy.10 = f32[2,2,32,1152]{3,2,1,0:T(8,128)} copy(f32[2,2,32,1152]{3,2,1,0:T(8,128)} %shard_map.73) | data formatting | bytes 1179648

commit v3 on v2

--- a/solution.py
+++ b/solution.py
@@ -140,9 +140,13 @@
             w_buf[q, 0, first : first + LANES, :] = (ur * er - ui * ei).astype(BF16)
             w_buf[q, 1, first : first + LANES, :] = (ur * ei + ui * er).astype(BF16)
 
-    early = tiles // 2
-    for t in range(early):
-        combine(t)
+    todo = list(range(tiles))
+
+    def combine_some(most):
+        for _ in range(min(most, len(todo))):
+            combine(todo.pop(0))
+
+    combine_some(0)
 
     pl.semaphore_wait(barrier, n - 1)
 
@@ -153,6 +157,7 @@
         )
 
     to_all(lambda p, b: q_copy(p, b, me).start())
+    combine_some(3)
 
     def q_done(p, b):
         q_copy(p, b, p * n_pb + b).wait_recv()
@@ -240,9 +245,9 @@
         if c >= 2:
             reduce(c - 2)
     for c in range(max(count - 2, 0), count):
+        combine_some(1)
         reduce(c)
-    for t in range(early, tiles):
-        combine(t)
+    combine_some(tiles)
 
     sums = [[0.0, 0.0] for _ in range(qd)]
     for c in range(count):

time: 36.8 us -> 34 us (0.924)
  Pallas kernels: 34 us -> 31.3 us
    pallas_call x1, Pallas kernels: 34 us -> 31.3 us  [body(): pl.pallas_call(functools.partial(kernel, cfg), out_shape=jax.ShapeDtypeSt...]
where the time goes in v3:
time: 34 us; the launch traced here: 33.8 us
  Pallas kernels  31.3 us (92%)
  local copies, waits for them, and re-layouts  1.92 us (6%)
  between operations  0.66 us (2%)
    pallas_call x1, Pallas kernels, body(): pl.pallas_call(functools.partial(kernel, cfg), out_shape=jax.ShapeDtypeSt...  31.3 us
    unnamed x1, local copies, waits for them, and re-layouts  1.92 us

profile of v3, /device:TPU:0, one launch (start us, length us, event | category | flops | bytes accessed | tf_op | source)
XLA Modules:
  0.0 33.8 jit_solution(11675192161857685563)
XLA Ops:
  0.7 31.3 %shard_map.73 = f32[2,2,32,1152]{3,2,1,0:T(8,128)} custom-call(bf16[2,512,2,1152]{3,2,1,0:T(2,128)(2,1)} %g_hbm.1, s32[3,1024]{1,0:T(4,128)} %rp_hbm.1, s32[2,3]{1,0:T(2,128)} %bitcast.3, s32[1]{0:T(128)S(6)} %copy.9.k_ref, bf16[8,2,32,32]{3,2,1,0:T(8,128)(2,1)} %kv_hbm.1, bf16[2,2,32,32]{3,2,1,0:T(8,128)(2,1)} %v_hbm.1, bf16[2,36,2,36]{3,2,1,0:T(2,128)(2,1)} %bitcast.2), custom_call_target="tpu_custom_call" | custom-call | tf_op jit(solution)/shard_map/pallas_call | solution.py:289
  31.9 1.9 %copy.10 = f32[2,2,32,1152]{3,2,1,0:T(8,128)} copy(f32[2,2,32,1152]{3,2,1,0:T(8,128)} %shard_map.73) | data formatting | bytes 1179648

commit v4 on v3

--- a/solution.py
+++ b/solution.py
@@ -245,7 +245,7 @@
         if c >= 2:
             reduce(c - 2)
     for c in range(max(count - 2, 0), count):
-        combine_some(1)
+        combine_some(1 + (c == count - 1))
         reduce(c)
     combine_some(tiles)
 

time: 34 us -> 34 us (level)
  no operation moved by 1% of the time
where the time goes in v4:
time: 34 us; the launch traced here: 33.8 us
  Pallas kernels  31.3 us (92%)
  local copies, waits for them, and re-layouts  1.92 us (6%)
  between operations  0.66 us (2%)
    pallas_call x1, Pallas kernels, body(): pl.pallas_call(functools.partial(kernel, cfg), out_shape=jax.ShapeDtypeSt...  31.3 us
    unnamed x1, local copies, waits for them, and re-layouts  1.92 us

profile of v4, /device:TPU:0, one launch (start us, length us, event | category | flops | bytes accessed | tf_op | source)
XLA Modules:
  0.0 33.8 jit_solution(15120369219207687664)
XLA Ops:
  0.7 31.3 %shard_map.73 = f32[2,2,32,1152]{3,2,1,0:T(8,128)} custom-call(bf16[2,512,2,1152]{3,2,1,0:T(2,128)(2,1)} %g_hbm.1, s32[3,1024]{1,0:T(4,128)} %rp_hbm.1, s32[2,3]{1,0:T(2,128)} %bitcast.3, s32[1]{0:T(128)S(6)} %copy.9.k_ref, bf16[8,2,32,32]{3,2,1,0:T(8,128)(2,1)} %kv_hbm.1, bf16[2,2,32,32]{3,2,1,0:T(8,128)(2,1)} %v_hbm.1, bf16[2,36,2,36]{3,2,1,0:T(2,128)(2,1)} %bitcast.2), custom_call_target="tpu_custom_call" | custom-call | tf_op jit(solution)/shard_map/pallas_call | solution.py:289
  31.9 1.9 %copy.10 = f32[2,2,32,1152]{3,2,1,0:T(8,128)} copy(f32[2,2,32,1152]{3,2,1,0:T(8,128)} %shard_map.73) | data formatting | bytes 1179648
